TPU v7x, 32 devices: a whole 2x2x4 slice. The times are simulated.
32 devices in a mesh: groups: 2 (over x), rows: 16 (over z, y, core).
Axes of the slice: x: 2, y: 2, z: 4, core: 2. Of those that a mesh axis runs over, the one named last changes fastest.
Arguments:
- queries: bfloat16 [2048, 8192], P(('groups', 'rows')), parts along dimension 0, may hold values from -6 to 6
- sketches: bfloat16 [16384, 8192], P(('groups', 'rows')), parts along dimension 0, may hold values from -16 to 16, as said below
- row_ids: int32 [16384], P(('groups', 'rows')), parts along dimension 0, may hold values from 0 to 8191, each once
Outputs:
- top_scores: float32 [2048, 128], P(('groups', 'rows')), parts along dimension 0
There are 2 independent parts, one for each index of `groups`. A program takes and returns all parts, laid end to end along the dimension named above; each array names one. Nothing has to cross between parts.
Inputs may be any that keep to these rules, and one draw needn't show every extreme that they name: `sketches`: sketch entries are real-valued.
All inputs are finite; a program needn't handle non-finite values.
Results may differ from a plain program's by a relative error of at most 0.0003.
Values may be sent and summed in bfloat16 or wider, within the bound.
A program may use at most 128 MiB of HBM per device.

v0:
```python
import jax
import jax.numpy as jnp
from jax import lax
from jax.sharding import PartitionSpec as P

TOPK = 128


def shards(queries, sketches, row_ids):
    devices = lax.axis_size("rows")
    total_rows = sketches.shape[0] * devices
    retired = total_rows // 4
    live_count = total_rows - retired
    keep = TOPK
    scores = lax.dot_general(
        lax.all_gather(queries, "rows", axis=0, tiled=True),
        sketches,
        (((1,), (1,)), ((), ())),
        preferred_element_type=jnp.float32,
    )
    live = row_ids >= retired
    square_sum = jnp.sum(jnp.where(live[None, :], scores * scores, jnp.float32(0.0)), axis=1)
    masked = jnp.where(live[None, :], scores, jnp.float32(-1e30))
    candidates = lax.top_k(masked, keep)[0]
    payload = (candidates, square_sum[:, None])
    received = (
        lax.all_to_all(payload[0], "rows", split_axis=0, concat_axis=1, tiled=True),
        lax.all_to_all(payload[1], "rows", split_axis=0, concat_axis=1, tiled=True),
    )
    best = lax.top_k(received[0], keep)[0]
    own_sum = jnp.sum(received[1], axis=1)
    inverse_scale = lax.rsqrt(own_sum / jnp.float32(live_count) + jnp.float32(1e-06))
    return best * inverse_scale[:, None]


def solution(mesh):
    return jax.shard_map(
        shards,
        mesh=mesh,
        in_specs=(P(("groups", "rows"), None), P(("groups", "rows"), None), P(("groups", "rows"))),
        out_specs=P(("groups", "rows"), None),
        check_vma=False,
    )
```

profile of v0, /device:TPU:0, one launch (start us, length us, event | category | flops | bytes accessed | tf_op | source)
XLA Modules:
  0.0 261.9 jit_solution(8203778866880331875)
XLA Ops:
  6.5 0.0 all-gather.2.cloned.1.call-start
  6.5 0.7 all-gather.2.cloned.1.call-update
  7.3 0.7 broadcast_compare_fusion
  7.9 130.7 %all-gather.2.cloned.1.call-done = bf16[1024,8192]{1,0:T(8,128)(2,1)} async-done(((bf16[64,8192]{1,0:T(8,128)(2,1)}), bf16[1024,8192]{1,0:T(8,128)(2,1)}) %all-gather.2.cloned.1.call-update) | async-done | bytes 16777232 | tf_op jit(solution)/shard_map/all_gather | solution.py:16
  138.7 15.9 %select_reduce_fusion = (f32[1024]{0:T(1024)S(1)}, f32[1024,512]{0,1:T(8,128)}) fusion(pred[512]{0:T(512)(128)(4,1)S(1)} %broadcast_compare_fusion, bf16[1024,8192]{1,0:T(8,128)(2,1)} %all-gather.2.cloned.1.call-done, bf16[512,8192]{1,0:T(8,128)(2,1)} %param.4), kind=kOutput, calls=%fused_computation | convolution fusion | flops 8592030720 | bytes 27267584 | tf_op jit(solution)/shard_map/dot_general | solution.py:15
  154.5 0.7 all_to_all.28
  155.2 3.5 %all-to-all-start.1 = ((f32[16,64,1]{1,2,0:T(1,128)}), f32[16,64,1]{1,2,0:T(1,128)S(1)}, u32[]{:S(2)}, u32[]{:S(2)}) async-start(f32[16,64,1]{1,2,0:T(1,128)} %bitcast.2), calls=%async_computation.1 | async-start | bytes 16384 | tf_op jit(solution)/shard_map/all_to_all | solution.py:28
  158.7 0.1 iota.6.clone
  158.8 58.5 %top_k.14 = (f32[1024,512]{0,1:T(8,128)}, s32[1024,512]{0,1:T(8,128)}) sort(f32[1024,512]{0,1:T(8,128)} %get-tuple-element.15, s32[1024,512]{0,1:T(8,128)S(1)} %iota.6.clone), dimensions={1}, to_apply=%region_0.1 | sort | flops 9961472 | bytes 8388608 | tf_op jit(solution)/shard_map/top_k | solution.py:24
  217.3 1.9 copy.11
  219.3 0.9 top_k.22
  220.1 0.0 all-to-all-done.1
  220.1 6.0 %all-to-all-start = ((f32[16,64,128]{2,1,0:T(8,128)}), f32[16,64,128]{2,1,0:T(8,128)S(1)}, u32[]{:S(2)}, u32[]{:S(2)}) async-start(f32[16,64,128]{2,1,0:T(8,128)} %bitcast), calls=%async_computation | async-start | bytes 1048576 | tf_op jit(solution)/shard_map/all_to_all | solution.py:27
  226.2 14.2 %all-to-all-done = f32[16,64,128]{2,1,0:T(8,128)S(1)} async-done(((f32[16,64,128]{2,1,0:T(8,128)}), f32[16,64,128]{2,1,0:T(8,128)S(1)}, u32[]{:S(2)}, u32[]{:S(2)}) %all-to-all-start) | async-done | bytes 524320 | tf_op jit(solution)/shard_map/all_to_all | solution.py:27
  240.4 14.0 %sort_prefixfusion = f32[64,128]{1,0:T(8,128)S(1)} fusion(f32[64,2048]{1,0:T(8,128)S(1)} %copy_bitcast_fusion), kind=kCustom, calls=%top_k.20.sort_prefix | custom fusion | flops 2228224 | bytes 557056 | tf_op jit(solution)/shard_map/top_k | solution.py:30
  254.4 0.7 broadcast_multiply_fusion
  (3 shorter events, 0.1 us)
Async XLA Ops:
  6.5 132.1 %all-gather.2.cloned.1.call-start = ((), (), s32[]{:S(2)}) async-start(), calls=%async_computation.2 | async-start | bytes 17825792 | tf_op jit(solution)/shard_map/all_gather | solution.py:16
  155.2 64.9 %all-to-all-start.1 = ((f32[16,64,1]{1,2,0:T(1,128)}), f32[16,64,1]{1,2,0:T(1,128)S(1)}, u32[]{:S(2)}, u32[]{:S(2)}) async-start(f32[16,64,1]{1,2,0:T(1,128)} %bitcast.2), calls=%async_computation.1 | async-start | bytes 16384 | tf_op jit(solution)/shard_map/all_to_all | solution.py:28
  220.1 20.2 %all-to-all-start = ((f32[16,64,128]{2,1,0:T(8,128)}), f32[16,64,128]{2,1,0:T(8,128)S(1)}, u32[]{:S(2)}, u32[]{:S(2)}) async-start(f32[16,64,128]{2,1,0:T(8,128)} %bitcast), calls=%async_computation | async-start | bytes 1048576 | tf_op jit(solution)/shard_map/all_to_all | solution.py:27
Sparse Core Ops, SparseCore 0:
  9.5 129.1 all-gather.1
where the time goes:
time: 262 us
  waiting for transfers between devices  146 us (56%)
  other arithmetic  73.9 us (28%)
  matrix products  15.9 us (6%)
  between operations  13.4 us (5%)
  starting transfers between devices  9.45 us (4%)
  local copies, waits for them, and re-layouts  3.62 us (1%)
    all_gather x1, waiting for transfers between devices, shards(): lax.all_gather(queries, 'rows', axis=0, tiled=True)  131 us
    top_k x1, other arithmetic, shards(): candidates = lax.top_k(masked, keep)[0]  58.5 us
    dot_general x1, matrix products, shards(): lax.dot_general(lax.all_gather(queries, 'rows', axis=0, tiled=True), sket...  15.9 us
    all_to_all x1, waiting for transfers between devices, shards(): lax.all_to_all(payload[0], 'rows', split_axis=0, concat_axis=1, tiled=True)  14.2 us
    top_k x1, other arithmetic, shards(): best = lax.top_k(received[0], keep)[0]  14 us
    all_to_all x1, starting transfers between devices, shards(): lax.all_to_all(payload[0], 'rows', split_axis=0, concat_axis=1, tiled=True)  5.98 us
  transfers between devices with their start and end apart: 3, of which 2 were waited for; matrix products, arithmetic and copies ran while one was open for 24% of the time, Pallas kernels for 0%

commit v1 on v0

--- a/solution.py
+++ b/solution.py
@@ -24,7 +24,12 @@
     candidates = lax.top_k(masked, keep)[0]
     payload = (candidates, square_sum[:, None])
     received = (
-        lax.all_to_all(payload[0], "rows", split_axis=0, concat_axis=1, tiled=True),
+        jnp.concatenate(
+            lax.all_to_all(
+                jnp.stack(jnp.split(payload[0], lax.axis_size("rows"), axis=0)), "rows", 0, 0
+            ),
+            axis=1,
+        ),
         lax.all_to_all(payload[1], "rows", split_axis=0, concat_axis=1, tiled=True),
     )
     best = lax.top_k(received[0], keep)[0]

time: 262 us -> 271 us (1.034)
  local copies, waits for them, and re-layouts: 3.62 us -> 12.5 us
    unnamed x0 -> x15, local copies, waits for them, and re-layouts: none -> 9.1 us
  transfers between devices with their start and end apart: 3 -> 3, of which waited for: 2 -> 2; matrix products, arithmetic and copies ran while one was open for 24% -> 26% of each run, Pallas kernels for 0% -> 0%
where the time goes in v1:
time: 271 us
  waiting for transfers between devices  146 us (54%)
  other arithmetic  73.9 us (27%)
  matrix products  15.9 us (6%)
  between operations  13.4 us (5%)
  local copies, waits for them, and re-layouts  12.5 us (5%)
  starting transfers between devices  9.45 us (3%)
    all_gather x1, waiting for transfers between devices, shards(): lax.all_gather(queries, 'rows', axis=0, tiled=True)  131 us
    top_k x1, other arithmetic, shards(): candidates = lax.top_k(masked, keep)[0]  58.5 us
    dot_general x1, matrix products, shards(): lax.dot_general(lax.all_gather(queries, 'rows', axis=0, tiled=True), sket...  15.9 us
    all_to_all x1, waiting for transfers between devices, shards(): lax.all_to_all(jnp.stack(jnp.split(payload[0], lax.axis_size('rows'), axi...  14.2 us
    top_k x1, other arithmetic, shards(): best = lax.top_k(received[0], keep)[0]  14 us
    unnamed x15, local copies, waits for them, and re-layouts  9.1 us
    all_to_all x1, starting transfers between devices, shards(): lax.all_to_all(jnp.stack(jnp.split(payload[0], lax.axis_size('rows'), axi...  5.98 us
  transfers between devices with their start and end apart: 3, of which 2 were waited for; matrix products, arithmetic and copies ran while one was open for 26% of the time, Pallas kernels for 0%

profile of v1, /device:TPU:0, one launch (start us, length us, event | category | flops | bytes accessed | tf_op | source)
XLA Modules:
  0.0 270.8 jit_solution(6565948817199451901)
XLA Ops:
  6.5 0.0 all-gather.2.cloned.1.call-start
  6.5 0.7 all-gather.2.cloned.1.call-update
  7.3 0.7 broadcast_compare_fusion
  7.9 130.7 %all-gather.2.cloned.1.call-done = bf16[1024,8192]{1,0:T(8,128)(2,1)} async-done(((bf16[64,8192]{1,0:T(8,128)(2,1)}), bf16[1024,8192]{1,0:T(8,128)(2,1)}) %all-gather.2.cloned.1.call-update) | async-done | bytes 16777232 | tf_op jit(solution)/shard_map/all_gather | solution.py:16
  138.7 15.9 %select_reduce_fusion = (f32[1024]{0:T(1024)S(1)}, f32[1024,512]{0,1:T(8,128)}) fusion(pred[512]{0:T(512)(128)(4,1)S(1)} %broadcast_compare_fusion, bf16[1024,8192]{1,0:T(8,128)(2,1)} %all-gather.2.cloned.1.call-done, bf16[512,8192]{1,0:T(8,128)(2,1)} %param.4), kind=kOutput, calls=%fused_computation | convolution fusion | flops 8592030720 | bytes 27267584 | tf_op jit(solution)/shard_map/dot_general | solution.py:15
  154.5 0.7 all_to_all.14
  155.2 3.5 %all-to-all-start.1 = ((f32[16,64,1]{1,2,0:T(1,128)}), f32[16,64,1]{1,2,0:T(1,128)S(1)}, u32[]{:S(2)}, u32[]{:S(2)}) async-start(f32[16,64,1]{1,2,0:T(1,128)} %bitcast.17), calls=%async_computation.1 | async-start | bytes 16384 | tf_op jit(solution)/shard_map/all_to_all | solution.py:33
  158.7 0.1 iota.6.clone
  158.8 58.5 %top_k.13 = (f32[1024,512]{0,1:T(8,128)}, s32[1024,512]{0,1:T(8,128)}) sort(f32[1024,512]{0,1:T(8,128)} %get-tuple-element.15, s32[1024,512]{0,1:T(8,128)S(1)} %iota.6.clone), dimensions={1}, to_apply=%region_0.1 | sort | flops 9961472 | bytes 8388608 | tf_op jit(solution)/shard_map/top_k | solution.py:24
  217.3 1.9 copy.11
  219.3 0.6 constant_dynamic-update-slice_fusion.15
  219.9 0.6 constant_dynamic-update-slice_fusion.14
  220.5 0.6 constant_dynamic-update-slice_fusion.13
  221.1 0.6 constant_dynamic-update-slice_fusion.12
  221.7 0.6 constant_dynamic-update-slice_fusion.11
  222.3 0.6 constant_dynamic-update-slice_fusion.10
  222.9 0.6 constant_dynamic-update-slice_fusion.9
  223.5 0.6 constant_dynamic-update-slice_fusion.8
  224.1 0.6 constant_dynamic-update-slice_fusion.7
  224.7 0.6 constant_dynamic-update-slice_fusion.6
  225.3 0.6 constant_dynamic-update-slice_fusion.5
  226.0 0.6 constant_dynamic-update-slice_fusion.4
  226.6 0.6 constant_dynamic-update-slice_fusion.3
  227.2 0.6 constant_dynamic-update-slice_fusion.2
  227.8 0.6 constant_dynamic-update-slice_fusion.1
  228.4 0.6 constant_dynamic-update-slice_fusion
  229.0 0.0 all-to-all-done.1
  229.0 6.0 %all-to-all-start = ((f32[16,64,128]{2,1,0:T(8,128)}), f32[16,64,128]{2,1,0:T(8,128)S(1)}, u32[]{:S(2)}, u32[]{:S(2)}) async-start(f32[16,64,128]{2,1,0:T(8,128)} %constant_dynamic-update-slice_fusion), calls=%async_computation | async-start | bytes 1048576 | tf_op jit(solution)/shard_map/all_to_all | solution.py:28
  235.0 14.2 %all-to-all-done = f32[16,64,128]{2,1,0:T(8,128)S(1)} async-done(((f32[16,64,128]{2,1,0:T(8,128)}), f32[16,64,128]{2,1,0:T(8,128)S(1)}, u32[]{:S(2)}, u32[]{:S(2)}) %all-to-all-start) | async-done | bytes 524320 | tf_op jit(solution)/shard_map/all_to_all | solution.py:28
  249.3 14.0 %sort_prefixfusion = f32[64,128]{1,0:T(8,128)S(1)} fusion(f32[64,2048]{1,0:T(8,128)S(1)} %copy_bitcast_fusion), kind=kCustom, calls=%top_k.14.sort_prefix | custom fusion | flops 2228224 | bytes 557056 | tf_op jit(solution)/shard_map/top_k | solution.py:35
  263.3 0.7 broadcast_multiply_fusion
  (3 shorter events, 0.1 us)
Async XLA Ops:
  6.5 132.1 %all-gather.2.cloned.1.call-start = ((), (), s32[]{:S(2)}) async-start(), calls=%async_computation.2 | async-start | bytes 17825792 | tf_op jit(solution)/shard_map/all_gather | solution.py:16
  155.2 73.8 %all-to-all-start.1 = ((f32[16,64,1]{1,2,0:T(1,128)}), f32[16,64,1]{1,2,0:T(1,128)S(1)}, u32[]{:S(2)}, u32[]{:S(2)}) async-start(f32[16,64,1]{1,2,0:T(1,128)} %bitcast.17), calls=%async_computation.1 | async-start | bytes 16384 | tf_op jit(solution)/shard_map/all_to_all | solution.py:33
  229.0 20.2 %all-to-all-start = ((f32[16,64,128]{2,1,0:T(8,128)}), f32[16,64,128]{2,1,0:T(8,128)S(1)}, u32[]{:S(2)}, u32[]{:S(2)}) async-start(f32[16,64,128]{2,1,0:T(8,128)} %constant_dynamic-update-slice_fusion), calls=%async_computation | async-start | bytes 1048576 | tf_op jit(solution)/shard_map/all_to_all | solution.py:28
Sparse Core Ops, SparseCore 0:
  9.5 129.1 all-gather.1
